TPU v7x, 128 devices: a whole 4x4x4 slice. The times are simulated.
128 devices in a mesh: seq: 8 (over z, core), head: 16 (over x, y).
Axes of the slice: x: 4, y: 4, z: 4, core: 2. Of those that a mesh axis runs over, the one named last changes fastest.
Arguments:
- lengths: int32 [16], replicated, may hold values from 128 to 8192, as said below
- page_owner: int32 [1536], replicated, may hold values from 0 to 16, as said below
- page_index: int32 [1536], replicated, may hold values from 0 to 127, as said below
- page_dest: int32 [1536], replicated, may hold values from 0 to 1535, as said below
- src_cache: bfloat16 [1536, 8, 64, 256], P(('seq', 'head')), may hold values from -8 to 8
- queries: bfloat16 [2, 16, 4096], replicated, may hold values from -8 to 8
- new_kv: bfloat16 [2, 16, 8, 256], replicated, may hold values from -6 to 6
- hidden_in: bfloat16 [2, 16, 4096], P(None, None, ('seq', 'head')), may hold values from -60 to 60
- out_weight: bfloat16 [4096, 4096], P(None, ('seq', 'head')), may hold values from -1.5 to 1.5
- norm_gain: bfloat16 [4096], P(('seq', 'head')), may hold values from 0.099609375 to 1.8984375
- router: bfloat16 [4096, 8], P(('seq', 'head')), may hold values from -0.09375 to 0.09375
- routes: int32 [2, 16, 2], replicated, may hold values from 0 to 7, all different within a row
- w_gate: bfloat16 [8, 4096, 8192], P('seq', None, 'head'), may hold values from -0.09375 to 0.09375
- w_up: bfloat16 [8, 4096, 8192], P('seq', None, 'head'), may hold values from -0.09375 to 0.09375
- w_down: bfloat16 [8, 8192, 4096], P('seq', 'head'), may hold values from -0.0625 to 0.0625
Outputs:
- page_pool: bfloat16 [16, 768, 64, 256], P('head', 'seq')
- mixed: bfloat16 [2, 16, 4096], P(None, None, ('seq', 'head'))
Inputs may be any that keep to these rules, and one draw needn't show every extreme that they name: Each length is at least 128; one equals 8192; the requests' pages, lengths[r] / 64 rounded up for request r, fit into the 1536 pages. `page_owner`: request r owns exactly lengths[r] / 64 rounded up source pages; the other pages carry 16. `page_index`: the pages of request r carry 0 to their count minus 1, each once; pages without request carry 0. `page_dest`: A permutation. Slot g belongs to destination group ((g % 768) // 96) * 2 + g // 768. Of the 12 pages that one device holds (pages i * 12 to (i + 1) * 12 - 1), at most 1 go to one group, and every draw has a device that sends exactly 1 to some group.
All inputs are finite; a program needn't handle non-finite values.
Results may differ from a plain program's by a relative error of at most 0.009.
Values may be sent and summed in bfloat16 or wider, within the bound.
A program may use at most 128 MiB of HBM per device.

v0:
```python
import jax
import jax.numpy as jnp
from jax import lax
from jax.sharding import Mesh
from jax.sharding import PartitionSpec as P

D = 4096
HQ = 32
KVH = 8
HD = 128
TOPK = 2
PAGE = 64
REQS = 16
SEQ = ("seq_0", "seq_1")
HEAD = ("head_0", "head_1")
SEQ_HEAD = ("seq_0", "seq_1", "head_0", "head_1")
NEG_FILL = -1e30
EPSILON = 1e-05
HIGHEST = lax.Precision.HIGHEST


def joined_all(array, axes, combine):
    for axis in axes:
        pieces = jax.tree.map(lambda part: lax.all_gather(part, axis), array)
        array = jax.tree.map(lambda part: part[0], pieces)
        for k in range(1, lax.axis_size(axis)):
            array = combine(array, jax.tree.map(lambda part: part[k], pieces))
    return array


def over_axes(array, axes):
    for axis in axes:
        array = lax.psum(array, axis)
    return array


def in_blocks(array, dim, peers):
    lengths = array.shape
    blocks = array.reshape(*lengths[:dim], peers, lengths[dim] // peers, *lengths[dim + 1 :])
    return jnp.moveaxis(blocks, dim, 0)


def cut_rows(length, count):
    unit = 8 if length >= 8 * count else 1
    return [length // unit * k // count * unit for k in range(1, count)]


def own_block(blocks, axes, sequence):
    lengths = [lax.axis_size(a) for a in axes]
    blocks = blocks.reshape(*lengths, *blocks.shape[1:])
    blocks = blocks.transpose(*sequence, *range(len(axes), blocks.ndim))
    blocks = blocks.reshape(-1, *blocks.shape[len(axes) :])
    for k in sequence:
        blocks = lax.psum_scatter(blocks, axes[k], scatter_dimension=0, tiled=True)
    return blocks[0]


def sum_all_axes_2(array, axes, dim):
    blocks = in_blocks(array, dim, lax.axis_size(axes))
    widest = max(range(1, max(2, blocks.ndim - 1)), key=lambda d: blocks.shape[d])
    count, gathered = (len(axes), [])
    for initial, share in enumerate(
        jnp.split(blocks, cut_rows(blocks.shape[widest], count), axis=widest)
    ):
        if share.size:
            sequence = [(initial + k) % count for k in range(count)]
            gathered.append(own_block(share, axes, sequence))
    return jnp.concatenate(gathered, axis=widest - 1)


def gate_mix(logits, picked):
    expert_ids = jnp.arange(logits.shape[1], dtype=jnp.int32)[None, :]
    first_hit = picked[:, 0:1] == expert_ids
    second_hit = picked[:, 1:2] == expert_ids
    first_logit = jnp.sum(jnp.where(first_hit, logits, 0.0), axis=1)
    second_logit = jnp.sum(jnp.where(second_hit, logits, 0.0), axis=1)
    leading = 1.0 / (1.0 + jnp.exp(second_logit - first_logit))
    trailing = 1.0 / (1.0 + jnp.exp(first_logit - second_logit))
    return jnp.where(first_hit, leading[:, None], 0.0) + jnp.where(
        second_hit, trailing[:, None], 0.0
    )


def combine(earlier, later):
    first_top, first_sum, first_acc = earlier
    second_top, second_sum, second_acc = later
    joint_top = jnp.maximum(first_top, second_top)
    first_factor = jnp.exp(first_top - joint_top)
    second_factor = jnp.exp(second_top - joint_top)
    return (
        joint_top,
        first_sum * first_factor + second_sum * second_factor,
        first_acc * first_factor[..., None] + second_acc * second_factor[..., None],
    )


def slot_plan(page_dest, pages_dev, slot_count, slots_dev, replicas, groups):
    part_index = page_dest // slot_count
    within = page_dest % slot_count
    target = within // slots_dev * replicas + part_index
    position = within % slots_dev
    per_device = target.reshape(-1, pages_dev)
    onehot = (per_device[:, :, None] == jnp.arange(groups, dtype=jnp.int32)[None, None, :]).astype(
        jnp.int32
    )
    before = jnp.cumsum(onehot, axis=1) - onehot
    ranking = jnp.sum(before * onehot, axis=2).reshape(-1)
    return (target, position, ranking)


def partial_attention(page_block, owners, page_pos, lengths, grouped, score_scale):
    head_dim = grouped.shape[-1]
    page_len = page_block.shape[2]
    requests = grouped.shape[1]
    clipped = jnp.minimum(owners, requests - 1)
    length_cap = jnp.take(lengths, clipped)
    offsets = page_pos[:, None] * page_len + jnp.arange(page_len, dtype=jnp.int32)[None, :]
    is_live = (owners < requests)[:, None] & (offsets < length_cap[:, None])
    live_mask = is_live[None, :, None, None, :]
    asked_rows = jnp.take(grouped, clipped, axis=1)
    scores = (
        jnp.einsum(
            "spkgd,pktd->spkgt",
            asked_rows,
            page_block[..., :head_dim],
            preferred_element_type=jnp.float32,
        )
        * score_scale
    )
    scores = jnp.where(live_mask, scores, NEG_FILL)
    members = owners[:, None] == jnp.arange(requests, dtype=jnp.int32)[None, :]
    page_top = jnp.max(scores, axis=4)
    row_top = jnp.max(
        jnp.where(members[None, :, :, None, None], page_top[:, :, None], NEG_FILL), axis=1
    )
    weights = jnp.where(
        live_mask, jnp.exp(scores - jnp.take(row_top, clipped, axis=1)[..., None]), 0.0
    )
    member_mask = members.astype(jnp.float32)
    totals = jnp.einsum("pr,spkg->srkg", member_mask, jnp.sum(weights, axis=4), precision=HIGHEST)
    page_out = jnp.einsum(
        "spkgt,pktd->spkgd",
        weights.astype(jnp.bfloat16),
        page_block[..., head_dim:],
        preferred_element_type=jnp.float32,
    )
    weighted = jnp.einsum("pr,spkgd->srkgd", member_mask, page_out, precision=HIGHEST)
    return (row_top, totals, weighted)


def body(
    lengths,
    page_owner,
    page_index,
    page_dest,
    src_cache,
    queries,
    new_kv,
    hidden_in,
    out_weight,
    norm_gain,
    router,
    routes,
    w_gate,
    w_up,
    w_down,
):
    seq_count = lax.axis_size(SEQ)
    head_count = lax.axis_size(HEAD)
    device_count = seq_count * head_count
    seq_pos = lax.axis_index(SEQ)
    head_pos = lax.axis_index(HEAD)
    pages_dev = src_cache.shape[0]
    page_total = page_dest.shape[0]
    replicas = head_count // KVH
    groups = seq_count * replicas
    slot_count = page_total // replicas
    slots_dev = pages_dev * KVH
    capacity = (slots_dev + device_count - 1) // device_count
    group_size = HQ // KVH
    step_count = queries.shape[0]
    row_count = step_count * REQS
    source = seq_pos * head_count + head_pos
    target, position, ranking = slot_plan(
        page_dest, pages_dev, slot_count, slots_dev, replicas, groups
    )
    local_target = lax.dynamic_slice_in_dim(target, source * pages_dev, pages_dev)
    local_rank = lax.dynamic_slice_in_dim(ranking, source * pages_dev, pages_dev)
    wanted = jnp.arange(groups * capacity, dtype=jnp.int32)
    matches = (local_target[None, :] == (wanted // capacity)[:, None]) & (
        local_rank[None, :] == (wanted % capacity)[:, None]
    )
    picked_page = jnp.sum(
        jnp.where(matches, jnp.arange(pages_dev, dtype=jnp.int32)[None, :], 0), axis=1
    )
    filled = jnp.any(matches, axis=1)
    packed = jnp.where(
        filled[:, None, None, None],
        jnp.take(src_cache, picked_page, axis=0),
        jnp.zeros((), jnp.bfloat16),
    )
    packed = packed.reshape(seq_count, replicas, capacity, KVH, PAGE, 2 * HD).transpose(
        0, 3, 1, 2, 4, 5
    )
    arrived = lax.all_to_all(
        packed.reshape(device_count, capacity, PAGE, 2 * HD),
        SEQ_HEAD,
        split_axis=0,
        concat_axis=0,
        tiled=True,
    )
    arrived = arrived.reshape(device_count * capacity, PAGE, 2 * HD)
    my_group = seq_pos * replicas + head_pos % replicas
    slot_ids = jnp.arange(slots_dev, dtype=jnp.int32)
    holders = (target[None, :] == my_group) & (position[None, :] == slot_ids[:, None])
    flat_index = jnp.arange(page_total, dtype=jnp.int32) // pages_dev * capacity + ranking
    chosen = jnp.sum(jnp.where(holders, flat_index[None, :], 0), axis=1)
    page_pool = jnp.take(arrived, chosen, axis=0)
    grouped = queries.reshape(step_count, REQS, KVH, group_size, HD)
    score_scale = HD ** (-0.5)
    kv_head = head_pos // replicas
    owners = jnp.sum(jnp.where(holders, page_owner[None, :], 0), axis=1)
    places = jnp.sum(jnp.where(holders, page_index[None, :], 0), axis=1)
    own_queries = lax.dynamic_slice_in_dim(grouped, kv_head, 1, axis=2)
    row_top, totals, weighted = partial_attention(
        page_pool[:, None], owners, places, lengths, own_queries, score_scale
    )
    owned_head = (jnp.arange(KVH, dtype=jnp.int32) == kv_head)[None, None, :, None]
    row_top = jnp.where(owned_head, row_top, NEG_FILL)
    totals = jnp.where(owned_head, totals, 0.0)
    weighted = jnp.where(owned_head[..., None], weighted, 0.0)
    row_top, totals, weighted = joined_all(
        (
            row_top.reshape(step_count, REQS, HQ),
            totals.reshape(step_count, REQS, HQ),
            weighted.reshape(step_count, REQS, HQ, HD),
        ),
        SEQ_HEAD,
        combine,
    )
    fresh_scores = (
        jnp.einsum(
            "srkgd,urkd->srkgu", grouped, new_kv[..., :HD], preferred_element_type=jnp.float32
        )
        * score_scale
    )
    causal = (jnp.arange(step_count)[:, None] >= jnp.arange(step_count)[None, :])[:, None, None, :]
    fresh_scores = jnp.where(
        causal, fresh_scores.reshape(step_count, REQS, HQ, step_count), NEG_FILL
    )
    joint_top = jnp.maximum(row_top, jnp.max(fresh_scores, axis=3))
    factor = jnp.exp(row_top - joint_top)
    fresh_weights = jnp.where(causal, jnp.exp(fresh_scores - joint_top[..., None]), 0.0)
    totals = totals * factor + jnp.sum(fresh_weights, axis=3)
    fresh_rounded = fresh_weights.reshape(step_count, REQS, KVH, group_size, step_count).astype(
        jnp.bfloat16
    )
    fresh_out = jnp.einsum(
        "srkgu,urkd->srkgd", fresh_rounded, new_kv[..., HD:], preferred_element_type=jnp.float32
    )
    weighted = weighted * factor[..., None] + fresh_out.reshape(step_count, REQS, HQ, HD)
    attended = (weighted / totals[..., None]).reshape(row_count, HQ * HD).astype(jnp.bfloat16)
    attn_out = jnp.dot(attended, out_weight, preferred_element_type=jnp.float32)
    middle = hidden_in.reshape(row_count, -1).astype(jnp.float32) + attn_out
    gain_row = norm_gain.astype(jnp.float32)[None, :]
    squares, routed = (
        over_axes(jnp.sum(middle * middle, axis=1), SEQ_HEAD),
        over_axes(
            jnp.dot(middle * gain_row, router.astype(jnp.float32), precision=HIGHEST), SEQ_HEAD
        ),
    )
    inverse_rms = lax.rsqrt(squares / D + EPSILON)
    logits = routed * inverse_rms[:, None]
    normed = (middle * inverse_rms[:, None] * gain_row).astype(jnp.bfloat16)
    features = lax.all_gather(normed, SEQ_HEAD, axis=1, tiled=True)
    mixture = gate_mix(logits, routes.reshape(row_count, TOPK))
    local_experts = w_gate.shape[0]
    local_mix = lax.dynamic_slice_in_dim(mixture, seq_pos * local_experts, local_experts, axis=1)
    gate_act = jnp.einsum("rd,edf->erf", features, w_gate, preferred_element_type=jnp.float32)
    upward = jnp.einsum("rd,edf->erf", features, w_up, preferred_element_type=jnp.float32)
    inner_act = (jax.nn.silu(gate_act) * upward).astype(jnp.bfloat16)
    produced = jnp.einsum("erf,efd->erd", inner_act, w_down, preferred_element_type=jnp.float32)
    moe_out = sum_all_axes_2(jnp.sum(local_mix.T[:, :, None] * produced, axis=0).T, SEQ_HEAD, 0)
    mixed = (middle + moe_out.T).astype(jnp.bfloat16).reshape(step_count, REQS, -1)
    return (page_pool[None], mixed)


def solution(mesh):
    split = Mesh(mesh.devices.reshape(4, 2, 4, 4), ("seq_0", "seq_1", "head_0", "head_1"))
    in_specs = (
        P(),
        P(),
        P(),
        P(),
        P(SEQ_HEAD, None, None, None),
        P(),
        P(),
        P(None, None, SEQ_HEAD),
        P(None, SEQ_HEAD),
        P(SEQ_HEAD),
        P(SEQ_HEAD, None),
        P(),
        P(SEQ, None, HEAD),
        P(SEQ, None, HEAD),
        P(SEQ, HEAD, None),
    )
    out_specs = (P(HEAD, SEQ, None, None), P(None, None, SEQ_HEAD))
    return jax.shard_map(body, mesh=split, in_specs=in_specs, out_specs=out_specs, check_vma=False)
```

profile of v0, /device:TPU:0, one launch (start us, length us, event | category | flops | bytes accessed | tf_op | source)
XLA Modules:
  0.0 609.9 jit_solution(12945465828086669318)
XLA Ops:
  9.1 2.7 gather_fusion
  11.9 2.7 select_bitcast_fusion
  14.6 2.3 copy.230
  16.9 11.7 %all-to-all-start = ((bf16[128,1,64,256]{3,2,1,0:T(8,128)(2,1)}), bf16[128,1,64,256]{3,2,1,0:T(8,128)(2,1)}, u32[]{:S(2)}, u32[]{:S(2)}) async-start(bf16[128,1,64,256]{3,2,1,0:T(8,128)(2,1)} %bitcast.483), calls=%async_computation | async-start | bytes 8388608 | tf_op jit(solution)/shard_map/all_to_all | solution.py:205
  31.8 9.8 %fusion.130 = (s32[96]{0:T(128)S(1)}, s32[96]{0:T(128)S(1)}) fusion(s32[]{:T(128)} %bitcast.17, s32[]{:T(128)} %bitcast.18, s32[]{:T(128)} %bitcast.19, s32[]{:T(128)} %bitcast.20, s32[]{:T(128)} %bitcast.21, s32[]{:T(128)} %bitcast.22, s32[]{:T(128)} %bitcast.23, s32[]{:T(128)} %bitcast.24, s32[]{:T(128)} %bitcast.25, s32[]{:T(128)} %bitcast.26, ...), kind=kLoop, calls=%fused_computation.273 | loop fusion | flops 4032 | bytes 1600 | tf_op jit(solution)/shard_map/jit(_take)/select_n | solution.py:116
  41.7 38.0 %all-to-all-done = bf16[128,1,64,256]{3,2,1,0:T(8,128)(2,1)} async-done(((bf16[128,1,64,256]{3,2,1,0:T(8,128)(2,1)}), bf16[128,1,64,256]{3,2,1,0:T(8,128)(2,1)}, u32[]{:S(2)}, u32[]{:S(2)}) %all-to-all-start) | async-done | bytes 4194336 | tf_op jit(solution)/shard_map/all_to_all | solution.py:205
  79.7 3.0 gather_fusion.1
  88.4 2.0 fusion.8
  92.8 12.2 %all_gather.49 = f32[4,2,16,32]{3,2,1,0:T(8,128)S(1)} all-gather(f32[1,2,16,32]{3,2,1,0:T(8,128)S(1)} %copy.236), channel_id=1, replica_groups=mesh['seq_0'=4,'seq_1'=2,'head_0'=4,'head_1'=4] {'seq_0'}, dimensions={0}, use_global_device_ids=true | all-gather | bytes 20480 | tf_op jit(solution)/shard_map/all_gather | solution.py:24
  105.0 14.8 %all-gather.5.cloned.1.call-done = f32[4,2,16,32,128]{4,3,2,1,0:T(8,128)} async-done(((f32[1,2,16,32,128]{4,3,2,1,0:T(8,128)}), f32[4,2,16,32,128]{4,3,2,1,0:T(8,128)}) %all-gather.5.cloned.1.call-update) | async-done | bytes 2097168 | tf_op jit(solution)/shard_map/all_gather | solution.py:24
  119.8 2.9 fusion.45
  122.8 12.0 %all_gather.56 = f32[4,2,16,32]{3,2,1,0:T(8,128)S(1)} all-gather(f32[1,2,16,32]{3,2,1,0:T(8,128)S(1)} %copy.255), channel_id=1, replica_groups=mesh['seq_0'=4,'seq_1'=2,'head_0'=4,'head_1'=4] {'seq_0'}, dimensions={0}, use_global_device_ids=true | all-gather | bytes 20480 | tf_op jit(solution)/shard_map/all_gather | solution.py:24
  136.7 2.3 fusion.44
  141.0 12.1 %all_gather.53 = f32[4,2,16,32]{3,2,1,0:T(8,128)S(1)} all-gather(f32[1,2,16,32]{3,2,1,0:T(8,128)S(1)} %get-tuple-element.32), channel_id=1, replica_groups=mesh['seq_0'=4,'seq_1'=2,'head_0'=4,'head_1'=4] {'head_0'}, dimensions={0}, use_global_device_ids=true | all-gather | bytes 20480 | tf_op jit(solution)/shard_map/all_gather | solution.py:24
  153.1 16.3 %all-gather.9.cloned.1.call-done = f32[4,2,16,32,128]{4,3,2,1,0:T(8,128)} async-done(((f32[1,2,16,32,128]{4,3,2,1,0:T(8,128)}), f32[4,2,16,32,128]{4,3,2,1,0:T(8,128)}) %all-gather.9.cloned.1.call-update) | async-done | bytes 2097168 | tf_op jit(solution)/shard_map/all_gather | solution.py:24
  169.5 2.9 fusion.39
  172.5 2.4 fusion.152
  175.3 11.9 %all_gather.58 = f32[4,2,16,32]{3,2,1,0:T(8,128)S(1)} all-gather(f32[1,2,16,32]{3,2,1,0:T(8,128)S(1)} %get-tuple-element.31), channel_id=1, replica_groups=mesh['seq_0'=4,'seq_1'=2,'head_0'=4,'head_1'=4] {'head_0'}, dimensions={0}, use_global_device_ids=true | all-gather | bytes 20480 | tf_op jit(solution)/shard_map/all_gather | solution.py:24
  187.1 13.0 %all_gather.55 = f32[4,2,16,32]{3,2,1,0:T(8,128)S(1)} all-gather(f32[1,2,16,32]{3,2,1,0:T(8,128)S(1)} %get-tuple-element.30), channel_id=1, replica_groups=mesh['seq_0'=4,'seq_1'=2,'head_0'=4,'head_1'=4] {'head_1'}, dimensions={0}, use_global_device_ids=true | all-gather | bytes 20480 | tf_op jit(solution)/shard_map/all_gather | solution.py:24
  201.5 11.9 %all_gather.59 = f32[4,2,16,32]{3,2,1,0:T(8,128)S(1)} all-gather(f32[1,2,16,32]{3,2,1,0:T(8,128)S(1)} %get-tuple-element.29), channel_id=1, replica_groups=mesh['seq_0'=4,'seq_1'=2,'head_0'=4,'head_1'=4] {'head_1'}, dimensions={0}, use_global_device_ids=true | all-gather | bytes 20480 | tf_op jit(solution)/shard_map/all_gather | solution.py:24
  218.5 3.6 multiply_reduce_fusion
  222.3 10.7 %all-reduce.6 = (f32[32]{0:T(128)S(1)}, f32[32,8]{0,1:T(8,128)S(1)}) all-reduce(f32[32]{0:T(128)S(1)} %get-tuple-element.95, f32[32,8]{0,1:T(8,128)S(1)} %fusion.112), channel_id=1, replica_groups=mesh['seq_0'=4,'seq_1'=2,'head_0'=4,'head_1'=4] {'seq_0'}, use_global_device_ids=true, to_apply=%region_17.18 | all-reduce | flops 288 | bytes 2304 | tf_op jit(solution)/shard_map/psum | solution.py:33
  233.0 2.5 all-reduce.7
  235.5 8.7 %all-reduce.5 = (f32[32]{0:T(128)S(1)}, f32[32,8]{0,1:T(8,128)S(1)}) all-reduce(f32[32]{0:T(128)S(1)} %get-tuple-element.15, f32[32,8]{0,1:T(8,128)S(1)} %get-tuple-element.16), channel_id=1, replica_groups=mesh['seq_0'=4,'seq_1'=2,'head_0'=4,'head_1'=4] {'head_0'}, use_global_device_ids=true, to_apply=%region_19.20 | all-reduce | flops 288 | bytes 2304 | tf_op jit(solution)/shard_map/psum | solution.py:33
  244.3 10.3 %all-reduce.4 = (f32[32]{0:T(128)S(1)}, f32[32,8]{0,1:T(8,128)S(1)}) all-reduce(f32[32]{0:T(128)S(1)} %get-tuple-element.11, f32[32,8]{0,1:T(8,128)S(1)} %get-tuple-element.12), channel_id=1, replica_groups=mesh['seq_0'=4,'seq_1'=2,'head_0'=4,'head_1'=4] {'head_1'}, use_global_device_ids=true, to_apply=%region_20.21 | all-reduce | flops 288 | bytes 2304 | tf_op jit(solution)/shard_map/psum | solution.py:33
  254.6 60.0 %all_gather.60 = bf16[32,4096]{0,1:T(8,128)(2,1)S(1)} all-gather(bf16[32,32]{0,1:T(8,128)(2,1)S(1)} %multiply_convert_fusion), channel_id=1, replica_groups=mesh['seq_0'=4,'seq_1'=2,'head_0'=4,'head_1'=4] {'seq_0','seq_1','head_0..., dimensions={1}, use_global_device_ids=true | all-gather | bytes 264192 | tf_op jit(solution)/shard_map/all_gather | solution.py:275
  314.7 3.0 fusion.14
  317.7 5.1 fusion
  323.5 4.9 fusion.144
  328.5 2.9 copy.267
  331.5 3.1 copy.266
  335.4 15.0 %reduce-scatter.31.cloned.1.call-done = f32[32,8,32]{2,1,0:T(8,128)} async-done(((f32[128,8,32]{2,1,0:T(8,128)}), f32[32,8,32]{2,1,0:T(8,128)}) %reduce-scatter.31.cloned.1.call-update) | async-done | bytes 32784 | tf_op jit(solution)/shard_map/reduce_scatter | solution.py:54
  350.4 23.5 %reduce-scatter.25.cloned.1.call-done = f32[32,8,32]{2,1,0:T(8,128)} async-done(((f32[128,8,32]{2,1,0:T(8,128)}), f32[32,8,32]{2,1,0:T(8,128)}) %reduce-scatter.25.cloned.1.call-update) | async-done | bytes 32784 | tf_op jit(solution)/shard_map/reduce_scatter | solution.py:54
  374.0 32.0 %reduce-scatter.13.cloned.1.call-done = f32[32,8,32]{1,0,2:T(8,128)} async-done(((f32[128,8,32]{1,0,2:T(8,128)}), f32[32,8,32]{1,0,2:T(8,128)}) %reduce-scatter.13.cloned.1.call-update) | async-done | bytes 32784 | tf_op jit(solution)/shard_map/reduce_scatter | solution.py:54
  408.2 20.8 %reduce-scatter.33.cloned.1.call-done = f32[8,8,32]{2,1,0:T(8,128)} async-done(((f32[32,8,32]{2,1,0:T(8,128)}), f32[8,8,32]{2,1,0:T(8,128)}) %reduce-scatter.33.cloned.1.call-update) | async-done | bytes 8208 | tf_op jit(solution)/shard_map/reduce_scatter | solution.py:54
  429.0 22.5 %reduce-scatter.27.cloned.1.call-done = f32[8,8,32]{2,1,0:T(8,128)} async-done(((f32[32,8,32]{2,1,0:T(8,128)}), f32[8,8,32]{2,1,0:T(8,128)}) %reduce-scatter.27.cloned.1.call-update) | async-done | bytes 8208 | tf_op jit(solution)/shard_map/reduce_scatter | solution.py:54
  454.1 9.8 %reduce-scatter.15.cloned.1.call-done = f32[16,8,32]{1,0,2:T(8,128)} async-done(((f32[32,8,32]{1,0,2:T(8,128)}), f32[16,8,32]{1,0,2:T(8,128)}) %reduce-scatter.15.cloned.1.call-update) | async-done | bytes 16400 | tf_op jit(solution)/shard_map/reduce_scatter | solution.py:54
  465.7 4.1 bitcast_select_fusion.1
  469.8 8.4 %reduce-scatter.19.cloned.1.call-done = f32[64,8,32]{2,1,0:T(8,128)} async-done(((f32[128,8,32]{2,1,0:T(8,128)}), f32[64,8,32]{2,1,0:T(8,128)}) %reduce-scatter.19.cloned.1.call-update) | async-done | bytes 65552 | tf_op jit(solution)/shard_map/reduce_scatter | solution.py:54
  478.3 13.6 %reduce-scatter.35.cloned.1.call-done = f32[4,8,32]{2,1,0:T(8,128)} async-done(((f32[8,8,32]{2,1,0:T(8,128)}), f32[4,8,32]{2,1,0:T(8,128)}) %reduce-scatter.35.cloned.1.call-update) | async-done | bytes 4112 | tf_op jit(solution)/shard_map/reduce_scatter | solution.py:54
  491.9 17.7 %all-reduce.3 = f32[4,8,32]{2,1,0:T(8,128)S(1)} all-reduce(f32[4,8,32]{2,1,0:T(8,128)} %reduce-scatter.35.cloned.1.call-done), channel_id=17, replica_groups=mesh['seq_0'=4,'seq_1'=2,'head_0'=4,'head_1'=4] {'head_0'}, use_global_device_ids=true, to_apply=%region_38.39.clone | all-reduce | flops 1024 | bytes 8192
  510.2 6.3 %reduce-scatter.29.cloned.1.call-done = f32[2,8,32]{2,1,0:T(8,128)} async-done(((f32[8,8,32]{2,1,0:T(8,128)}), f32[2,8,32]{2,1,0:T(8,128)}) %reduce-scatter.29.cloned.1.call-update) | async-done | bytes 2064 | tf_op jit(solution)/shard_map/reduce_scatter | solution.py:54
  516.5 2.6 all-reduce.2
  519.8 19.1 %reduce-scatter.17.cloned.1.call-done = f32[4,8,32]{2,1,0:T(8,128)} async-done(((f32[16,8,32]{2,1,0:T(8,128)}), f32[4,8,32]{2,1,0:T(8,128)}) %reduce-scatter.17.cloned.1.call-update) | async-done | bytes 4112 | tf_op jit(solution)/shard_map/reduce_scatter | solution.py:54
  538.8 17.5 %all-reduce = f32[4,8,32]{2,1,0:T(8,128)S(1)} all-reduce(f32[4,8,32]{2,1,0:T(8,128)} %reduce-scatter.17.cloned.1.call-done), channel_id=5, replica_groups=mesh['seq_0'=4,'seq_1'=2,'head_0'=4,'head_1'=4] {'head_1'}, use_global_device_ids=true, to_apply=%region_26.27.clone | all-reduce | flops 1024 | bytes 8192
  556.4 5.3 reduce-scatter.21.cloned.1.call-done
  562.3 22.0 %reduce-scatter.23.cloned.1.call-done = f32[4,8,32]{2,1,0:T(8,128)} async-done(((f32[16,8,32]{2,1,0:T(8,128)}), f32[4,8,32]{2,1,0:T(8,128)}) %reduce-scatter.23.cloned.1.call-update) | async-done | bytes 4112 | tf_op jit(solution)/shard_map/reduce_scatter | solution.py:54
  584.3 17.7 %all-reduce.1 = f32[4,8,32]{2,1,0:T(8,128)S(1)} all-reduce(f32[4,8,32]{2,1,0:T(8,128)} %reduce-scatter.23.cloned.1.call-done), channel_id=9, replica_groups=mesh['seq_0'=4,'seq_1'=2,'head_0'=4,'head_1'=4] {'seq_0'}, use_global_device_ids=true, to_apply=%region_30.31.clone | all-reduce | flops 1024 | bytes 8192
  (201 shorter events, 35.8 us)
Async XLA Ops:
  7.2 2.0 copy-start
  16.9 11.8 %copy-start.6 = (bf16[2,16,4096]{2,1,0:T(8,128)(2,1)S(1)}, bf16[2,16,4096]{2,1,0:T(8,128)(2,1)}, u32[]{:S(2)}) copy-start(bf16[2,16,4096]{2,1,0:T(8,128)(2,1)} %param.20) | copy-start | bytes 786436
  16.9 12.2 %copy-start.10 = (s32[1536]{0:T(1024)S(1)}, s32[1536]{0:T(1024)}, u32[]{:S(2)}) copy-start(s32[1536]{0:T(1024)} %param.18) | copy-start | bytes 18436
  16.9 12.2 %copy-start.12 = (s32[1536]{0:T(1024)S(1)}, s32[1536]{0:T(1024)}, u32[]{:S(2)}) copy-start(s32[1536]{0:T(1024)} %param.17) | copy-start | bytes 18436
  16.9 12.2 %copy-start.13 = (s32[1536]{0:T(1024)S(1)}, s32[1536]{0:T(1024)}, u32[]{:S(2)}) copy-start(s32[1536]{0:T(1024)} %param.16) | copy-start | bytes 18436
  16.9 14.2 %copy-start.9 = (s32[16]{0:T(128)S(1)}, s32[16]{0:T(128)}, u32[]{:S(2)}) copy-start(s32[16]{0:T(128)} %param.15) | copy-start | bytes 196
  16.9 62.8 %all-to-all-start = ((bf16[128,1,64,256]{3,2,1,0:T(8,128)(2,1)}), bf16[128,1,64,256]{3,2,1,0:T(8,128)(2,1)}, u32[]{:S(2)}, u32[]{:S(2)}) async-start(bf16[128,1,64,256]{3,2,1,0:T(8,128)(2,1)} %bitcast.483), calls=%async_computation | async-start | bytes 8388608 | tf_op jit(solution)/shard_map/all_to_all | solution.py:205
  28.6 91.2 %all-gather.5.cloned.1.call-start = ((), (), s32[]{:S(2)}) async-start(), calls=%async_computation.13 | async-start | bytes 2621440 | tf_op jit(solution)/shard_map/all_gather | solution.py:24
  82.7 1.7 copy-start.2
  82.7 3.3 copy-start.7
  84.3 1.7 copy-start.4
  91.7 45.0 %all-gather.7.cloned.1.call-start = ((), (), s32[]{:S(2)}) async-start(), calls=%async_computation.14 | async-start | bytes 1572864 | tf_op jit(solution)/shard_map/all_gather | solution.py:24
  122.7 49.7 %copy-start.11 = (bf16[2,16,32]{2,1,0:T(8,128)(2,1)S(1)}, bf16[2,16,32]{2,1,0:T(8,128)(2,1)}, u32[]{:S(2)}) copy-start(bf16[2,16,32]{2,1,0:T(8,128)(2,1)} %param.22) | copy-start | bytes 6148
  122.7 46.8 %all-gather.9.cloned.1.call-start = ((), (), s32[]{:S(2)}) async-start(), calls=%async_computation.15 | async-start | bytes 2621440 | tf_op jit(solution)/shard_map/all_gather | solution.py:24
  122.8 49.7 %copy-start.8 = (bf16[2,16,8,256]{3,2,1,0:T(8,128)(2,1)S(1)}, bf16[2,16,8,256]{3,2,1,0:T(8,128)(2,1)}, u32[]{:S(2)}) copy-start(bf16[2,16,8,256]{3,2,1,0:T(8,128)(2,1)} %param.21) | copy-start | bytes 393220
  139.1 36.1 %copy-start.16 = (bf16[32]{0:T(256)(128)(2,1)S(1)}, bf16[32]{0:T(256)(128)(2,1)}, u32[]{:S(2)}) copy-start(bf16[32]{0:T(256)(128)(2,1)} %param.24) | copy-start | bytes 196
  139.1 36.0 %copy-start.14 = (s32[2,16,2]{1,2,0:T(2,128)S(1)}, s32[2,16,2]{1,2,0:T(2,128)}, u32[]{:S(2)}) copy-start(s32[2,16,2]{1,2,0:T(2,128)} %param.26) | copy-start | bytes 772
  139.1 76.0 %all-gather.11.cloned.1.call-start = ((), (), s32[]{:S(2)}) async-start(), calls=%async_computation.16 | async-start | bytes 2621440 | tf_op jit(solution)/shard_map/all_gather | solution.py:24
  172.3 178.0 %reduce-scatter.31.cloned.1.call-start = ((), (), s32[]{:S(2)}) async-start(), calls=%async_computation.26 | async-start | bytes 655360 | tf_op jit(solution)/shard_map/reduce_scatter | solution.py:54
  216.9 1.6 copy-start.5
  218.5 3.6 copy-start.15
  331.4 74.7 %copy-start.3 = (f32[128,8,32]{1,0,2:T(8,128)S(1)}, f32[128,8,32]{1,0,2:T(8,128)}, u32[]{:S(2)}) copy-start(f32[128,8,32]{1,0,2:T(8,128)} %get-tuple-element.40) | copy-start | bytes 393220
  331.4 42.6 %reduce-scatter.25.cloned.1.call-start = ((), (), s32[]{:S(2)}) async-start(), calls=%async_computation.23 | async-start | bytes 655360 | tf_op jit(solution)/shard_map/reduce_scatter | solution.py:54
  334.5 117.1 %copy-start.20 = (u32[128]{0:T(128)S(1)}, u32[128]{0:T(128)}, u32[]{:S(2)}) copy-start(u32[128]{0:T(128)} %constant.244) | copy-start | bytes 1540
  334.6 117.7 %copy-start.19 = (u32[128]{0:T(128)S(1)}, u32[128]{0:T(128)}, u32[]{:S(2)}) copy-start(u32[128]{0:T(128)} %constant.240) | copy-start | bytes 1540
  334.6 118.3 %copy-start.18 = (u32[128]{0:T(128)S(1)}, u32[128]{0:T(128)}, u32[]{:S(2)}) copy-start(u32[128]{0:T(128)} %constant.236) | copy-start | bytes 1540
  334.6 118.9 %copy-start.17 = (u32[128]{0:T(128)S(1)}, u32[128]{0:T(128)}, u32[]{:S(2)}) copy-start(u32[128]{0:T(128)} %constant.232) | copy-start | bytes 1540
  334.6 71.5 %reduce-scatter.13.cloned.1.call-start = ((), (), s32[]{:S(2)}) async-start(), calls=%async_computation.17 | async-start | bytes 2621440 | tf_op jit(solution)/shard_map/reduce_scatter | solution.py:54
  335.3 93.6 %reduce-scatter.33.cloned.1.call-start = ((), (), s32[]{:S(2)}) async-start(), calls=%async_computation.27 | async-start | bytes 163840 | tf_op jit(solution)/shard_map/reduce_scatter | solution.py:54
  350.4 101.2 %reduce-scatter.27.cloned.1.call-start = ((), (), s32[]{:S(2)}) async-start(), calls=%async_computation.24 | async-start | bytes 163840 | tf_op jit(solution)/shard_map/reduce_scatter | solution.py:54
  374.0 89.9 %reduce-scatter.15.cloned.1.call-start = ((), (), s32[]{:S(2)}) async-start(), calls=%async_computation.18 | async-start | bytes 786432 | tf_op jit(solution)/shard_map/reduce_scatter | solution.py:54
  406.1 72.1 %reduce-scatter.19.cloned.1.call-start = ((), (), s32[]{:S(2)}) async-start(), calls=%async_computation.20 | async-start | bytes 786432 | tf_op jit(solution)/shard_map/reduce_scatter | solution.py:54
  408.1 83.8 %reduce-scatter.35.cloned.1.call-start = ((), (), s32[]{:S(2)}) async-start(), calls=%async_computation.28 | async-start | bytes 49152 | tf_op jit(solution)/shard_map/reduce_scatter | solution.py:54
  429.0 87.6 %reduce-scatter.29.cloned.1.call-start = ((), (), s32[]{:S(2)}) async-start(), calls=%async_computation.25 | async-start | bytes 40960 | tf_op jit(solution)/shard_map/reduce_scatter | solution.py:54
  451.6 87.3 %reduce-scatter.17.cloned.1.call-start = ((), (), s32[]{:S(2)}) async-start(), calls=%async_computation.19 | async-start | bytes 81920 | tf_op jit(solution)/shard_map/reduce_scatter | solution.py:54
  465.7 137.7 %copy-start.1 = (bf16[12,8,64,256]{3,2,1,0:T(8,128)(2,1)S(1)}, bf16[12,8,64,256]{3,2,1,0:T(8,128)(2,1)}, u32[]{:S(2)}) copy-start(bf16[12,8,64,256]{3,2,1,0:T(8,128)(2,1)} %param.19) | copy-start | bytes 9437188
  465.7 96.0 %reduce-scatter.21.cloned.1.call-start = ((), (), s32[]{:S(2)}) async-start(), calls=%async_computation.21 | async-start | bytes 327680 | tf_op jit(solution)/shard_map/reduce_scatter | solution.py:54
  478.2 106.0 %reduce-scatter.23.cloned.1.call-start = ((), (), s32[]{:S(2)}) async-start(), calls=%async_computation.22 | async-start | bytes 81920 | tf_op jit(solution)/shard_map/reduce_scatter | solution.py:54
Sparse Core Ops, SparseCore 0:
  91.8 27.9 all-gather.4
  122.8 11.3 all-gather.6
  139.2 30.1 all-gather.8
  172.5 31.3 all-gather.10
  331.5 18.7 reduce-scatter.30
  352.6 21.3 reduce-scatter.24
  376.4 29.6 reduce-scatter.12
  408.4 20.4 reduce-scatter.32
  431.3 20.1 reduce-scatter.26
  453.7 10.1 reduce-scatter.14
  466.3 11.8 reduce-scatter.18
  480.4 11.5 reduce-scatter.34
  494.3 22.2 reduce-scatter.28
  518.7 20.0 reduce-scatter.16
  541.1 20.5 reduce-scatter.20
  563.9 20.3 reduce-scatter.22
where the time goes:
time: 611 us; the launch traced here: 610 us
  waiting for transfers between devices  268 us (44%)
  blocking collectives  224 us (37%)
  local copies, waits for them, and re-layouts  42 us (7%)
  other arithmetic  29.7 us (5%)
  matrix products  18.5 us (3%)
  between operations  14.7 us (2%)
  starting transfers between devices  12.4 us (2%)
    reduce_scatter x12, waiting for transfers between devices, own_block(): blocks = lax.psum_scatter(blocks, axes[k], scatter_dimension=0, tiled=True)  198 us
    all_gather x8, blocking collectives, joined_all(): pieces = jax.tree.map(lambda part: lax.all_gather(part, axis), array)  76.6 us
    all_gather x1, blocking collectives, body(): features = lax.all_gather(normed, SEQ_HEAD, axis=1, tiled=True)  60 us
    unnamed x4, blocking collectives  55.5 us
    all_to_all x1, waiting for transfers between devices, body(): lax.all_to_all(packed.reshape(device_count, capacity, PAGE, 2 * HD), SEQ_...  38 us
    psum x4, blocking collectives, over_axes(): array = lax.psum(array, axis)  32.2 us
    all_gather x4, waiting for transfers between devices, joined_all(): pieces = jax.tree.map(lambda part: lax.all_gather(part, axis), array)  31.1 us
  transfers between devices with their start and end apart: 17, of which 15 were waited for; matrix products, arithmetic and copies ran while one was open for 6% of the time, Pallas kernels for 0%

commit v1 on v0

--- a/solution.py
+++ b/solution.py
@@ -272,7 +272,9 @@
     inverse_rms = lax.rsqrt(squares / D + EPSILON)
     logits = routed * inverse_rms[:, None]
     normed = (middle * inverse_rms[:, None] * gain_row).astype(jnp.bfloat16)
-    features = lax.all_gather(normed, SEQ_HEAD, axis=1, tiled=True)
+    features = jnp.concatenate(
+        lax.all_to_all(jnp.stack([normed] * lax.axis_size(SEQ_HEAD)), SEQ_HEAD, 0, 0), axis=1
+    )
     mixture = gate_mix(logits, routes.reshape(row_count, TOPK))
     local_experts = w_gate.shape[0]
     local_mix = lax.dynamic_slice_in_dim(mixture, seq_pos * local_experts, local_experts, axis=1)

time: 611 us -> 569 us (0.931)
  blocking collectives: 224 us -> 164 us
  waiting for transfers between devices: 268 us -> 278 us
    all_gather x1 -> x0, blocking collectives: 60 us -> none  [body(): features = lax.all_gather(normed, SEQ_HEAD, axis=1, tiled=True)]
    all_to_all x0 -> x1, waiting for transfers between devices: none -> 10.5 us  [body(): lax.all_to_all(jnp.stack([normed] * lax.axis_size(SEQ_HEAD)), SEQ_HEAD, 0...]
  transfers between devices with their start and end apart: 17 -> 18, of which waited for: 15 -> 16; matrix products, arithmetic and copies ran while one was open for 6% -> 6% of each run, Pallas kernels for 0% -> 0%
where the time goes in v1:
time: 569 us; the launch traced here: 568 us
  waiting for transfers between devices  278 us (49%)
  blocking collectives  164 us (29%)
  local copies, waits for them, and re-layouts  45.7 us (8%)
  other arithmetic  29.7 us (5%)
  matrix products  18.5 us (3%)
  starting transfers between devices  17.2 us (3%)
  between operations  14.7 us (3%)
    reduce_scatter x12, waiting for transfers between devices, own_block(): blocks = lax.psum_scatter(blocks, axes[k], scatter_dimension=0, tiled=True)  197 us
    all_gather x8, blocking collectives, joined_all(): pieces = jax.tree.map(lambda part: lax.all_gather(part, axis), array)  76.6 us
    unnamed x4, blocking collectives  55.4 us
    all_to_all x1, waiting for transfers between devices, body(): lax.all_to_all(packed.reshape(device_count, capacity, PAGE, 2 * HD), SEQ_...  38 us
    psum x4, blocking collectives, over_axes(): array = lax.psum(array, axis)  32.2 us
    all_gather x4, waiting for transfers between devices, joined_all(): pieces = jax.tree.map(lambda part: lax.all_gather(part, axis), array)  31.1 us
    all_to_all x1, starting transfers between devices, body(): lax.all_to_all(packed.reshape(device_count, capacity, PAGE, 2 * HD), SEQ_...  11.7 us
  transfers between devices with their start and end apart: 18, of which 16 were waited for; matrix products, arithmetic and copies ran while one was open for 6% of the time, Pallas kernels for 0%

profile of v1, /device:TPU:0, one launch (start us, length us, event | category | flops | bytes accessed | tf_op | source)
XLA Modules:
  0.0 567.7 jit_solution(5347149212515532319)
XLA Ops:
  9.1 2.7 gather_fusion
  11.9 2.7 select_bitcast_fusion
  14.6 2.3 copy.239
  16.9 11.7 %all-to-all-start = ((bf16[128,1,64,256]{3,2,1,0:T(8,128)(2,1)}), bf16[128,1,64,256]{3,2,1,0:T(8,128)(2,1)}, u32[]{:S(2)}, u32[]{:S(2)}) async-start(bf16[128,1,64,256]{3,2,1,0:T(8,128)(2,1)} %bitcast.484), calls=%async_computation | async-start | bytes 8388608 | tf_op jit(solution)/shard_map/all_to_all | solution.py:205
  31.8 9.8 %fusion.130 = (s32[96]{0:T(128)S(1)}, s32[96]{0:T(128)S(1)}) fusion(s32[]{:T(128)} %bitcast.17, s32[]{:T(128)} %bitcast.18, s32[]{:T(128)} %bitcast.19, s32[]{:T(128)} %bitcast.20, s32[]{:T(128)} %bitcast.21, s32[]{:T(128)} %bitcast.22, s32[]{:T(128)} %bitcast.23, s32[]{:T(128)} %bitcast.24, s32[]{:T(128)} %bitcast.25, s32[]{:T(128)} %bitcast.26, ...), kind=kLoop, calls=%fused_computation.273 | loop fusion | flops 4032 | bytes 1600 | tf_op jit(solution)/shard_map/jit(_take)/select_n | solution.py:116
  41.7 38.0 %all-to-all-done = bf16[128,1,64,256]{3,2,1,0:T(8,128)(2,1)} async-done(((bf16[128,1,64,256]{3,2,1,0:T(8,128)(2,1)}), bf16[128,1,64,256]{3,2,1,0:T(8,128)(2,1)}, u32[]{:S(2)}, u32[]{:S(2)}) %all-to-all-start) | async-done | bytes 4194336 | tf_op jit(solution)/shard_map/all_to_all | solution.py:205
  79.7 3.0 gather_fusion.1
  92.8 12.2 %all_gather.46 = f32[4,2,16,32]{3,2,1,0:T(8,128)S(1)} all-gather(f32[1,2,16,32]{3,2,1,0:T(8,128)S(1)} %copy.245), channel_id=1, replica_groups=mesh['seq_0'=4,'seq_1'=2,'head_0'=4,'head_1'=4] {'seq_0'}, dimensions={0}, use_global_device_ids=true | all-gather | bytes 20480 | tf_op jit(solution)/shard_map/all_gather | solution.py:24
  105.0 14.8 %all-gather.5.cloned.1.call-done = f32[4,2,16,32,128]{4,3,2,1,0:T(8,128)} async-done(((f32[1,2,16,32,128]{4,3,2,1,0:T(8,128)}), f32[4,2,16,32,128]{4,3,2,1,0:T(8,128)}) %all-gather.5.cloned.1.call-update) | async-done | bytes 2097168 | tf_op jit(solution)/shard_map/all_gather | solution.py:24
  119.8 2.9 fusion.45
  122.8 12.0 %all_gather.53 = f32[4,2,16,32]{3,2,1,0:T(8,128)S(1)} all-gather(f32[1,2,16,32]{3,2,1,0:T(8,128)S(1)} %copy.264), channel_id=1, replica_groups=mesh['seq_0'=4,'seq_1'=2,'head_0'=4,'head_1'=4] {'seq_0'}, dimensions={0}, use_global_device_ids=true | all-gather | bytes 20480 | tf_op jit(solution)/shard_map/all_gather | solution.py:24
  136.7 2.3 fusion.44
  141.0 12.1 %all_gather.50 = f32[4,2,16,32]{3,2,1,0:T(8,128)S(1)} all-gather(f32[1,2,16,32]{3,2,1,0:T(8,128)S(1)} %get-tuple-element.32), channel_id=1, replica_groups=mesh['seq_0'=4,'seq_1'=2,'head_0'=4,'head_1'=4] {'head_0'}, dimensions={0}, use_global_device_ids=true | all-gather | bytes 20480 | tf_op jit(solution)/shard_map/all_gather | solution.py:24
  153.1 16.3 %all-gather.9.cloned.1.call-done = f32[4,2,16,32,128]{4,3,2,1,0:T(8,128)} async-done(((f32[1,2,16,32,128]{4,3,2,1,0:T(8,128)}), f32[4,2,16,32,128]{4,3,2,1,0:T(8,128)}) %all-gather.9.cloned.1.call-update) | async-done | bytes 2097168 | tf_op jit(solution)/shard_map/all_gather | solution.py:24
  169.5 2.9 fusion.39
  172.5 2.4 fusion.152
  175.2 11.9 %all_gather.55 = f32[4,2,16,32]{3,2,1,0:T(8,128)S(1)} all-gather(f32[1,2,16,32]{3,2,1,0:T(8,128)S(1)} %get-tuple-element.31), channel_id=1, replica_groups=mesh['seq_0'=4,'seq_1'=2,'head_0'=4,'head_1'=4] {'head_0'}, dimensions={0}, use_global_device_ids=true | all-gather | bytes 20480 | tf_op jit(solution)/shard_map/all_gather | solution.py:24
  187.1 12.8 %all_gather.52 = f32[4,2,16,32]{3,2,1,0:T(8,128)S(1)} all-gather(f32[1,2,16,32]{3,2,1,0:T(8,128)S(1)} %get-tuple-element.30), channel_id=1, replica_groups=mesh['seq_0'=4,'seq_1'=2,'head_0'=4,'head_1'=4] {'head_1'}, dimensions={0}, use_global_device_ids=true | all-gather | bytes 20480 | tf_op jit(solution)/shard_map/all_gather | solution.py:24
  201.3 12.0 %all_gather.56 = f32[4,2,16,32]{3,2,1,0:T(8,128)S(1)} all-gather(f32[1,2,16,32]{3,2,1,0:T(8,128)S(1)} %get-tuple-element.29), channel_id=1, replica_groups=mesh['seq_0'=4,'seq_1'=2,'head_0'=4,'head_1'=4] {'head_1'}, dimensions={0}, use_global_device_ids=true | all-gather | bytes 20480 | tf_op jit(solution)/shard_map/all_gather | solution.py:24
  218.5 3.6 multiply_reduce_fusion
  222.3 10.7 %all-reduce.6 = (f32[32]{0:T(128)S(1)}, f32[32,8]{0,1:T(8,128)S(1)}) all-reduce(f32[32]{0:T(128)S(1)} %get-tuple-element.95, f32[32,8]{0,1:T(8,128)S(1)} %fusion.112), channel_id=1, replica_groups=mesh['seq_0'=4,'seq_1'=2,'head_0'=4,'head_1'=4] {'seq_0'}, use_global_device_ids=true, to_apply=%region_17.18 | all-reduce | flops 288 | bytes 2304 | tf_op jit(solution)/shard_map/psum | solution.py:33
  233.0 2.5 all-reduce.7
  235.5 8.7 %all-reduce.5 = (f32[32]{0:T(128)S(1)}, f32[32,8]{0,1:T(8,128)S(1)}) all-reduce(f32[32]{0:T(128)S(1)} %get-tuple-element.15, f32[32,8]{0,1:T(8,128)S(1)} %get-tuple-element.16), channel_id=1, replica_groups=mesh['seq_0'=4,'seq_1'=2,'head_0'=4,'head_1'=4] {'head_0'}, use_global_device_ids=true, to_apply=%region_19.20 | all-reduce | flops 288 | bytes 2304 | tf_op jit(solution)/shard_map/psum | solution.py:33
  244.2 10.3 %all-reduce.4 = (f32[32]{0:T(128)S(1)}, f32[32,8]{0,1:T(8,128)S(1)}) all-reduce(f32[32]{0:T(128)S(1)} %get-tuple-element.11, f32[32,8]{0,1:T(8,128)S(1)} %get-tuple-element.12), channel_id=1, replica_groups=mesh['seq_0'=4,'seq_1'=2,'head_0'=4,'head_1'=4] {'head_1'}, use_global_device_ids=true, to_apply=%region_20.21 | all-reduce | flops 288 | bytes 2304 | tf_op jit(solution)/shard_map/psum | solution.py:33
  256.3 4.6 all-to-all-start.1
  261.3 10.5 %all-to-all-done.1 = bf16[128,2,512]{2,1,0:T(2,128)(2,1)S(1)} async-done(((bf16[128,2,512]{2,1,0:T(2,128)(2,1)}), bf16[128,2,512]{2,1,0:T(2,128)(2,1)S(1)}, u32[]{:S(2)}, u32[]{:S(2)}) %all-to-all-start.1) | async-done | bytes 262176 | tf_op jit(solution)/shard_map/all_to_all | solution.py:276
  273.8 3.0 fusion.14
  276.8 5.1 fusion
  282.6 4.9 fusion.144
  287.5 2.9 copy.278
  290.6 3.1 copy.277
  294.5 13.7 %reduce-scatter.31.cloned.1.call-done = f32[32,8,32]{2,1,0:T(8,128)} async-done(((f32[128,8,32]{2,1,0:T(8,128)}), f32[32,8,32]{2,1,0:T(8,128)}) %reduce-scatter.31.cloned.1.call-update) | async-done | bytes 32784 | tf_op jit(solution)/shard_map/reduce_scatter | solution.py:54
  308.2 23.5 %reduce-scatter.25.cloned.1.call-done = f32[32,8,32]{2,1,0:T(8,128)} async-done(((f32[128,8,32]{2,1,0:T(8,128)}), f32[32,8,32]{2,1,0:T(8,128)}) %reduce-scatter.25.cloned.1.call-update) | async-done | bytes 32784 | tf_op jit(solution)/shard_map/reduce_scatter | solution.py:54
  331.8 32.0 %reduce-scatter.13.cloned.1.call-done = f32[32,8,32]{1,0,2:T(8,128)} async-done(((f32[128,8,32]{1,0,2:T(8,128)}), f32[32,8,32]{1,0,2:T(8,128)}) %reduce-scatter.13.cloned.1.call-update) | async-done | bytes 32784 | tf_op jit(solution)/shard_map/reduce_scatter | solution.py:54
  365.9 20.8 %reduce-scatter.33.cloned.1.call-done = f32[8,8,32]{2,1,0:T(8,128)} async-done(((f32[32,8,32]{2,1,0:T(8,128)}), f32[8,8,32]{2,1,0:T(8,128)}) %reduce-scatter.33.cloned.1.call-update) | async-done | bytes 8208 | tf_op jit(solution)/shard_map/reduce_scatter | solution.py:54
  386.8 22.5 %reduce-scatter.27.cloned.1.call-done = f32[8,8,32]{2,1,0:T(8,128)} async-done(((f32[32,8,32]{2,1,0:T(8,128)}), f32[8,8,32]{2,1,0:T(8,128)}) %reduce-scatter.27.cloned.1.call-update) | async-done | bytes 8208 | tf_op jit(solution)/shard_map/reduce_scatter | solution.py:54
  411.9 9.8 %reduce-scatter.15.cloned.1.call-done = f32[16,8,32]{1,0,2:T(8,128)} async-done(((f32[32,8,32]{1,0,2:T(8,128)}), f32[16,8,32]{1,0,2:T(8,128)}) %reduce-scatter.15.cloned.1.call-update) | async-done | bytes 16400 | tf_op jit(solution)/shard_map/reduce_scatter | solution.py:54
  423.5 4.1 bitcast_select_fusion.1
  427.6 8.4 %reduce-scatter.19.cloned.1.call-done = f32[64,8,32]{2,1,0:T(8,128)} async-done(((f32[128,8,32]{2,1,0:T(8,128)}), f32[64,8,32]{2,1,0:T(8,128)}) %reduce-scatter.19.cloned.1.call-update) | async-done | bytes 65552 | tf_op jit(solution)/shard_map/reduce_scatter | solution.py:54
  436.1 13.6 %reduce-scatter.35.cloned.1.call-done = f32[4,8,32]{2,1,0:T(8,128)} async-done(((f32[8,8,32]{2,1,0:T(8,128)}), f32[4,8,32]{2,1,0:T(8,128)}) %reduce-scatter.35.cloned.1.call-update) | async-done | bytes 4112 | tf_op jit(solution)/shard_map/reduce_scatter | solution.py:54
  449.7 17.6 %all-reduce.3 = f32[4,8,32]{2,1,0:T(8,128)S(1)} all-reduce(f32[4,8,32]{2,1,0:T(8,128)} %reduce-scatter.35.cloned.1.call-done), channel_id=17, replica_groups=mesh['seq_0'=4,'seq_1'=2,'head_0'=4,'head_1'=4] {'head_0'}, use_global_device_ids=true, to_apply=%region_38.39.clone | all-reduce | flops 1024 | bytes 8192
  468.0 6.3 %reduce-scatter.29.cloned.1.call-done = f32[2,8,32]{2,1,0:T(8,128)} async-done(((f32[8,8,32]{2,1,0:T(8,128)}), f32[2,8,32]{2,1,0:T(8,128)}) %reduce-scatter.29.cloned.1.call-update) | async-done | bytes 2064 | tf_op jit(solution)/shard_map/reduce_scatter | solution.py:54
  474.3 2.6 all-reduce.2
  477.6 19.1 %reduce-scatter.17.cloned.1.call-done = f32[4,8,32]{2,1,0:T(8,128)} async-done(((f32[16,8,32]{2,1,0:T(8,128)}), f32[4,8,32]{2,1,0:T(8,128)}) %reduce-scatter.17.cloned.1.call-update) | async-done | bytes 4112 | tf_op jit(solution)/shard_map/reduce_scatter | solution.py:54
  496.7 17.5 %all-reduce = f32[4,8,32]{2,1,0:T(8,128)S(1)} all-reduce(f32[4,8,32]{2,1,0:T(8,128)} %reduce-scatter.17.cloned.1.call-done), channel_id=5, replica_groups=mesh['seq_0'=4,'seq_1'=2,'head_0'=4,'head_1'=4] {'head_1'}, use_global_device_ids=true, to_apply=%region_26.27.clone | all-reduce | flops 1024 | bytes 8192
  514.2 5.3 reduce-scatter.21.cloned.1.call-done
  520.1 22.0 %reduce-scatter.23.cloned.1.call-done = f32[4,8,32]{2,1,0:T(8,128)} async-done(((f32[16,8,32]{2,1,0:T(8,128)}), f32[4,8,32]{2,1,0:T(8,128)}) %reduce-scatter.23.cloned.1.call-update) | async-done | bytes 4112 | tf_op jit(solution)/shard_map/reduce_scatter | solution.py:54
  542.0 17.7 %all-reduce.1 = f32[4,8,32]{2,1,0:T(8,128)S(1)} all-reduce(f32[4,8,32]{2,1,0:T(8,128)} %reduce-scatter.23.cloned.1.call-done), channel_id=9, replica_groups=mesh['seq_0'=4,'seq_1'=2,'head_0'=4,'head_1'=4] {'seq_0'}, use_global_device_ids=true, to_apply=%region_30.31.clone | all-reduce | flops 1024 | bytes 8192
  (208 shorter events, 41.8 us)
Async XLA Ops:
  7.2 2.0 copy-start
  16.9 11.8 %copy-start.6 = (bf16[2,16,4096]{2,1,0:T(8,128)(2,1)S(1)}, bf16[2,16,4096]{2,1,0:T(8,128)(2,1)}, u32[]{:S(2)}) copy-start(bf16[2,16,4096]{2,1,0:T(8,128)(2,1)} %param.20) | copy-start | bytes 786436
  16.9 12.2 %copy-start.10 = (s32[1536]{0:T(1024)S(1)}, s32[1536]{0:T(1024)}, u32[]{:S(2)}) copy-start(s32[1536]{0:T(1024)} %param.18) | copy-start | bytes 18436
  16.9 12.2 %copy-start.12 = (s32[1536]{0:T(1024)S(1)}, s32[1536]{0:T(1024)}, u32[]{:S(2)}) copy-start(s32[1536]{0:T(1024)} %param.17) | copy-start | bytes 18436
  16.9 12.2 %copy-start.13 = (s32[1536]{0:T(1024)S(1)}, s32[1536]{0:T(1024)}, u32[]{:S(2)}) copy-start(s32[1536]{0:T(1024)} %param.16) | copy-start | bytes 18436
  16.9 14.2 %copy-start.9 = (s32[16]{0:T(128)S(1)}, s32[16]{0:T(128)}, u32[]{:S(2)}) copy-start(s32[16]{0:T(128)} %param.15) | copy-start | bytes 196
  16.9 62.8 %all-to-all-start = ((bf16[128,1,64,256]{3,2,1,0:T(8,128)(2,1)}), bf16[128,1,64,256]{3,2,1,0:T(8,128)(2,1)}, u32[]{:S(2)}, u32[]{:S(2)}) async-start(bf16[128,1,64,256]{3,2,1,0:T(8,128)(2,1)} %bitcast.484), calls=%async_computation | async-start | bytes 8388608 | tf_op jit(solution)/shard_map/all_to_all | solution.py:205
  28.6 91.2 %all-gather.5.cloned.1.call-start = ((), (), s32[]{:S(2)}) async-start(), calls=%async_computation.14 | async-start | bytes 2621440 | tf_op jit(solution)/shard_map/all_gather | solution.py:24
  82.7 1.7 copy-start.2
  82.7 3.3 copy-start.7
  84.3 1.7 copy-start.4
  91.7 45.0 %all-gather.7.cloned.1.call-start = ((), (), s32[]{:S(2)}) async-start(), calls=%async_computation.15 | async-start | bytes 1572864 | tf_op jit(solution)/shard_map/all_gather | solution.py:24
  122.7 49.7 %copy-start.11 = (bf16[2,16,32]{2,1,0:T(8,128)(2,1)S(1)}, bf16[2,16,32]{2,1,0:T(8,128)(2,1)}, u32[]{:S(2)}) copy-start(bf16[2,16,32]{2,1,0:T(8,128)(2,1)} %param.22) | copy-start | bytes 6148
  122.7 46.8 %all-gather.9.cloned.1.call-start = ((), (), s32[]{:S(2)}) async-start(), calls=%async_computation.16 | async-start | bytes 2621440 | tf_op jit(solution)/shard_map/all_gather | solution.py:24
  122.8 49.6 %copy-start.8 = (bf16[2,16,8,256]{3,2,1,0:T(8,128)(2,1)S(1)}, bf16[2,16,8,256]{3,2,1,0:T(8,128)(2,1)}, u32[]{:S(2)}) copy-start(bf16[2,16,8,256]{3,2,1,0:T(8,128)(2,1)} %param.21) | copy-start | bytes 393220
  139.1 36.0 %copy-start.16 = (bf16[32]{0:T(256)(128)(2,1)S(1)}, bf16[32]{0:T(256)(128)(2,1)}, u32[]{:S(2)}) copy-start(bf16[32]{0:T(256)(128)(2,1)} %param.24) | copy-start | bytes 196
  139.1 36.0 %copy-start.14 = (s32[2,16,2]{1,2,0:T(2,128)S(1)}, s32[2,16,2]{1,2,0:T(2,128)}, u32[]{:S(2)}) copy-start(s32[2,16,2]{1,2,0:T(2,128)} %param.26) | copy-start | bytes 772
  139.1 75.9 %all-gather.11.cloned.1.call-start = ((), (), s32[]{:S(2)}) async-start(), calls=%async_computation.17 | async-start | bytes 2621440 | tf_op jit(solution)/shard_map/all_gather | solution.py:24
  216.8 1.6 copy-start.5
  218.5 3.6 copy-start.15
  256.3 15.5 %all-to-all-start.1 = ((bf16[128,2,512]{2,1,0:T(2,128)(2,1)}), bf16[128,2,512]{2,1,0:T(2,128)(2,1)S(1)}, u32[]{:S(2)}, u32[]{:S(2)}) async-start(bf16[128,2,512]{2,1,0:T(2,128)(2,1)} %reshape.896), calls=%async_computation.1 | async-start | bytes 524288 | tf_op jit(solution)/shard_map/all_to_all | solution.py:276
  260.9 47.2 %reduce-scatter.31.cloned.1.call-start = ((), (), s32[]{:S(2)}) async-start(), calls=%async_computation.27 | async-start | bytes 655360 | tf_op jit(solution)/shard_map/reduce_scatter | solution.py:54
  290.5 73.4 %copy-start.3 = (f32[128,8,32]{1,0,2:T(8,128)S(1)}, f32[128,8,32]{1,0,2:T(8,128)}, u32[]{:S(2)}) copy-start(f32[128,8,32]{1,0,2:T(8,128)} %get-tuple-element.40) | copy-start | bytes 393220
  290.5 41.2 %reduce-scatter.25.cloned.1.call-start = ((), (), s32[]{:S(2)}) async-start(), calls=%async_computation.24 | async-start | bytes 655360 | tf_op jit(solution)/shard_map/reduce_scatter | solution.py:54
  293.6 115.8 %copy-start.20 = (u32[128]{0:T(128)S(1)}, u32[128]{0:T(128)}, u32[]{:S(2)}) copy-start(u32[128]{0:T(128)} %constant.244) | copy-start | bytes 1540
  293.7 116.4 %copy-start.19 = (u32[128]{0:T(128)S(1)}, u32[128]{0:T(128)}, u32[]{:S(2)}) copy-start(u32[128]{0:T(128)} %constant.240) | copy-start | bytes 1540
  293.7 117.0 %copy-start.18 = (u32[128]{0:T(128)S(1)}, u32[128]{0:T(128)}, u32[]{:S(2)}) copy-start(u32[128]{0:T(128)} %constant.236) | copy-start | bytes 1540
  293.7 117.6 %copy-start.17 = (u32[128]{0:T(128)S(1)}, u32[128]{0:T(128)}, u32[]{:S(2)}) copy-start(u32[128]{0:T(128)} %constant.232) | copy-start | bytes 1540
  293.7 70.2 %reduce-scatter.13.cloned.1.call-start = ((), (), s32[]{:S(2)}) async-start(), calls=%async_computation.18 | async-start | bytes 2621440 | tf_op jit(solution)/shard_map/reduce_scatter | solution.py:54
  294.4 92.3 %reduce-scatter.33.cloned.1.call-start = ((), (), s32[]{:S(2)}) async-start(), calls=%async_computation.28 | async-start | bytes 163840 | tf_op jit(solution)/shard_map/reduce_scatter | solution.py:54
  308.2 101.2 %reduce-scatter.27.cloned.1.call-start = ((), (), s32[]{:S(2)}) async-start(), calls=%async_computation.25 | async-start | bytes 163840 | tf_op jit(solution)/shard_map/reduce_scatter | solution.py:54
  331.8 90.0 %reduce-scatter.15.cloned.1.call-start = ((), (), s32[]{:S(2)}) async-start(), calls=%async_computation.19 | async-start | bytes 786432 | tf_op jit(solution)/shard_map/reduce_scatter | solution.py:54
  363.9 72.2 %reduce-scatter.19.cloned.1.call-start = ((), (), s32[]{:S(2)}) async-start(), calls=%async_computation.21 | async-start | bytes 786432 | tf_op jit(solution)/shard_map/reduce_scatter | solution.py:54
  365.9 83.8 %reduce-scatter.35.cloned.1.call-start = ((), (), s32[]{:S(2)}) async-start(), calls=%async_computation.29 | async-start | bytes 49152 | tf_op jit(solution)/shard_map/reduce_scatter | solution.py:54
  386.8 87.6 %reduce-scatter.29.cloned.1.call-start = ((), (), s32[]{:S(2)}) async-start(), calls=%async_computation.26 | async-start | bytes 40960 | tf_op jit(solution)/shard_map/reduce_scatter | solution.py:54
  409.4 87.3 %reduce-scatter.17.cloned.1.call-start = ((), (), s32[]{:S(2)}) async-start(), calls=%async_computation.20 | async-start | bytes 81920 | tf_op jit(solution)/shard_map/reduce_scatter | solution.py:54
  423.5 137.7 %copy-start.1 = (bf16[12,8,64,256]{3,2,1,0:T(8,128)(2,1)S(1)}, bf16[12,8,64,256]{3,2,1,0:T(8,128)(2,1)}, u32[]{:S(2)}) copy-start(bf16[12,8,64,256]{3,2,1,0:T(8,128)(2,1)} %param.19) | copy-start | bytes 9437188
  423.5 96.0 %reduce-scatter.21.cloned.1.call-start = ((), (), s32[]{:S(2)}) async-start(), calls=%async_computation.22 | async-start | bytes 327680 | tf_op jit(solution)/shard_map/reduce_scatter | solution.py:54
  436.1 106.0 %reduce-scatter.23.cloned.1.call-start = ((), (), s32[]{:S(2)}) async-start(), calls=%async_computation.23 | async-start | bytes 81920 | tf_op jit(solution)/shard_map/reduce_scatter | solution.py:54
Sparse Core Ops, SparseCore 0:
  91.8 27.9 all-gather.4
  122.8 11.3 all-gather.6
  139.2 30.1 all-gather.8
  172.5 31.3 all-gather.10
  290.6 17.4 reduce-scatter.30
  310.4 21.3 reduce-scatter.24
  334.2 29.6 reduce-scatter.12
  366.2 20.4 reduce-scatter.32
  389.1 20.1 reduce-scatter.26
  411.5 10.1 reduce-scatter.14
  424.1 11.8 reduce-scatter.18
  438.2 11.5 reduce-scatter.34
  452.1 22.2 reduce-scatter.28
  476.5 20.0 reduce-scatter.16
  498.9 20.5 reduce-scatter.20
  521.7 20.3 reduce-scatter.22
